TPU v7x, 32 devices: a whole 2x2x4 slice. The times are simulated.
32 devices in a mesh: cuts: 8 (over z, x), mode: 4 (over y, core).
Axes of the slice: x: 2, y: 2, z: 4, core: 2. Of those that a mesh axis runs over, the one named last changes fastest.
Arguments:
- sliced_state: bfloat16 [8, 16, 4, 128, 2, 128], P(None, 'cuts', None, 'mode'), may hold values from -0.75 to 0.75
- gate_blocks: bfloat16 [32, 2, 128, 128], P('cuts'), may hold values from -0.375 to 0.375
- gate_slot: int32 [32], replicated, may hold values from 0 to 31, each once
- samples: int32 [8, 4096], replicated, may hold values from 0 to 65535
Outputs:
- amplitudes: float32 [32, 128, 2, 128], P('cuts', 'mode')
- sample_probs: float32 [8, 4096], replicated
- xeb_score: float32 [8], replicated
Inputs may be any that keep to these rules, and one draw needn't show every extreme that they name: `gate_slot`: a permutation: every gate block has its own row of gate_blocks. `samples`: flat index s * 128 * 128 + p * 128 + q.
All inputs are finite; a program needn't handle non-finite values.
Results may differ from a plain program's by a relative error of at most 0.022.
Values may be sent and summed in bfloat16 or wider, within the bound.
A program may use at most 64 MiB of HBM per device.

v0:
```python
import jax
import jax.numpy as jnp
from jax import lax
from jax.sharding import PartitionSpec as P


def from_root(array, axis, root):
    mine = lax.axis_index(axis) == root
    return lax.psum(jnp.where(mine, array, jnp.zeros_like(array)), axis)


def apply_gates(tensor, blocks):
    real_part = blocks[:, 0]
    imag_part = blocks[:, 1]
    stacked = jnp.concatenate(
        [
            jnp.concatenate([real_part, imag_part], axis=2),
            jnp.concatenate([-imag_part, real_part], axis=2),
        ],
        axis=1,
    )
    layout = tensor.shape
    flattened = tensor.reshape(layout[0], -1, 2 * layout[-1])
    product = jnp.einsum("crk,ckn->crn", flattened, stacked, preferred_element_type=jnp.float32)
    return product.astype(jnp.bfloat16).reshape(layout)


def select_rows(table, wanted):
    count = table.shape[0]
    onehot = (wanted[:, None] == jnp.arange(count, dtype=jnp.int32)[None, :]).astype(table.dtype)
    picked = jnp.dot(onehot, table.reshape(count, -1), preferred_element_type=jnp.float32)
    return picked.astype(table.dtype).reshape((wanted.shape[0],) + table.shape[1:])


def on_device(sliced_state, gate_blocks, gate_slot, samples):
    circuits = sliced_state.shape[0]
    spectator = sliced_state.shape[2]
    width = sliced_state.shape[5]
    held_count = gate_blocks.shape[0]
    layer_count = gate_slot.shape[0] // (2 * circuits)
    circuit_ids = jnp.arange(circuits, dtype=jnp.int32)
    tensor = lax.all_to_all(sliced_state, "mode", split_axis=0, concat_axis=3, tiled=True)
    local_count = tensor.shape[0]
    local_ids = lax.axis_index("mode") * local_count + jnp.arange(local_count, dtype=jnp.int32)

    def fetch_one(position):
        held_block = select_rows(gate_blocks, jnp.reshape(position % held_count, (1,)))[0]
        return from_root(held_block, "cuts", position // held_count)

    def fetch_gates(layer_index, gate_kind):
        fetched = []
        for circuit in range(local_count):
            fetched.append(
                fetch_one(
                    gate_slot[(local_ids[circuit] * layer_count + layer_index) * 2 + gate_kind]
                )
            )
        return jnp.stack(fetched, axis=0)

    for layer_index in range(layer_count):
        tensor = apply_gates(tensor, fetch_gates(layer_index, 0))
        tensor = jnp.swapaxes(tensor, 3, 5)
        tensor = apply_gates(tensor, fetch_gates(layer_index, 1))
        tensor = jnp.swapaxes(tensor, 3, 5)
    summed = jnp.sum(tensor.astype(jnp.float32), axis=1)
    summed = lax.all_to_all(
        summed.astype(jnp.bfloat16), "mode", split_axis=2, concat_axis=0, tiled=True
    ).astype(summed.dtype)
    local_rows = summed.shape[2]
    summed = summed.reshape(circuits * spectator, local_rows, 2, width)
    amplitudes = lax.psum_scatter(
        summed.astype(jnp.bfloat16), "cuts", scatter_dimension=0, tiled=True
    ).astype(jnp.float32)
    row_count = amplitudes.shape[0]
    first_row = lax.axis_index("cuts") * row_count
    first_col = lax.axis_index("mode") * local_rows
    magnitude = amplitudes[:, :, 0, :] ** 2 + amplitudes[:, :, 1, :] ** 2
    row_sums = jnp.sum(magnitude, axis=(1, 2))
    owner_circuit = (first_row + jnp.arange(row_count, dtype=jnp.int32)) // spectator
    norm_part = jnp.sum(
        jnp.where(owner_circuit[None, :] == circuit_ids[:, None], row_sums[None, :], 0.0), axis=1
    )
    plane_size = width * width
    spec_index = samples // plane_size
    row_index = samples // width % width
    col_index = samples % width
    local_row = circuit_ids[:, None] * spectator + spec_index - first_row
    local_col = row_index - first_col
    is_owned = (
        (local_row >= 0) & (local_row < row_count) & (local_col >= 0) & (local_col < local_rows)
    )
    cell_index = jnp.where(is_owned, local_row * local_rows + local_col, -1)
    cell_count = row_count * local_rows
    cell_onehot = (
        cell_index[:, :, None] == jnp.arange(cell_count, dtype=jnp.int32)[None, None, :]
    ).astype(jnp.float32)
    picked_rows = jnp.einsum(
        "csr,rw->csw",
        cell_onehot,
        magnitude.reshape(cell_count, width),
        precision=lax.Precision.HIGHEST,
    )
    col_match = col_index[:, :, None] == jnp.arange(width, dtype=jnp.int32)[None, None, :]
    sample_mass = jnp.sum(jnp.where(col_match, picked_rows, 0.0), axis=2)
    dimension_scale = float(spectator * plane_size)
    norm_total = lax.psum(norm_part, ("cuts", "mode"))
    sample_probs = lax.psum(sample_mass * dimension_scale / norm_total[:, None], ("cuts", "mode"))
    xeb_score = jnp.mean(sample_probs, axis=1)
    return (amplitudes, sample_probs, xeb_score)


def solution(mesh):
    in_specs = (P(None, "cuts", None, "mode", None, None), P("cuts", None, None, None), P(), P())
    out_specs = (P("cuts", "mode", None, None), P(), P())
    return jax.shard_map(
        on_device, mesh=mesh, in_specs=in_specs, out_specs=out_specs, check_vma=False
    )
```

profile of v0, /device:TPU:0, one launch (start us, length us, event | category | flops | bytes accessed | tf_op | source)
XLA Modules:
  0.0 402.5 jit_solution(14701239896464762398)
XLA Ops:
  10.4 1.6 fusion.73
  32.4 1.2 copy.56
  33.9 0.7 copy.39
  35.0 0.7 copy.40
  41.5 4.3 %all-to-all-start = ((bf16[8,2,4,32,2,128]{5,4,3,2,1,0:T(2,128)(2,1)}), bf16[8,2,4,32,2,128]{5,4,3,2,1,0:T(2,128)(2,1)S(1)}, u32[]{:S(2)}, u32[]{:S(2)}) async-start(bf16[8,2,4,32,2,128]{5,4,3,2,1,0:T(2,128)(2,1)} %param.4), calls=%async_computation | async-start | bytes 2097152 | tf_op jit(solution)/shard_map/all_to_all | solution.py:42
  45.8 72.8 %all-reduce.6.cloned.1.call-done = (bf16[1,2,128,128]{2,3,0,1:T(8,128)(2,1)}, bf16[1,2,128,128]{2,3,0,1:T(8,128)(2,1)}, bf16[1,2,128,128]{3,2,0,1:T(8,128)(2,1)}...) async-done(((bf16[1,2,128,128]{2,3,0,1:T(8,128)(2,1)}, ...) | async-done | bytes 524304 | tf_op jit(solution)/shard_map/psum | solution.py:9
  118.6 0.9 constant_dynamic-update-slice_fusion.1
  119.5 0.9 constant_dynamic-update-slice_fusion
  120.4 0.8 constant_dynamic-update-slice_fusion.3
  121.2 0.8 constant_dynamic-update-slice_fusion.5
  122.1 0.9 constant_dynamic-update-slice_fusion.2
  123.1 1.2 copy.55
  124.4 0.7 reshape.305
  125.5 0.8 reshape.306
  126.3 1.1 copy.42
  127.4 0.7 reshape.307
  128.9 1.2 copy.43
  130.1 0.7 reshape.309
  131.5 1.2 copy.44
  132.8 0.7 reshape.311
  134.2 2.4 reduce_sum.50
  136.7 0.7 copy.45
  137.4 11.4 %all_to_all.33 = bf16[2,4,128,2,128]{4,3,1,0,2:T(2,128)(2,1)S(1)} all-to-all(bf16[2,4,128,2,128]{4,3,1,0,2:T(2,128)(2,1)S(1)} %copy.45), channel_id=1, replica_groups=mesh['cuts'=8,'mode'=4] {'mode'}, dimensions={2} | all-to-all | bytes 1048576 | tf_op jit(solution)/shard_map/all_to_all | solution.py:66
  148.9 0.8 copy.47
  149.9 61.7 %reduce-scatter.2.cloned.1.call-done = bf16[4,32,2,128]{3,1,2,0:T(8,128)(2,1)} async-done(((bf16[32,32,2,128]{3,1,2,0:T(8,128)(2,1)}), bf16[4,32,2,128]{3,1,2,0:T(8,128)(2,1)}) %reduce-scatter.2.cloned.1.call-update) | async-done | bytes 65552 | tf_op jit(solution)/shard_map/reduce_scatter | solution.py:71
  211.5 0.8 convert_element_type.77
  212.9 40.1 %psum.78 = f32[8]{0:T(128)S(1)} all-reduce(f32[8]{0:T(128)S(1)} %select_reduce_fusion.1), channel_id=1, replica_groups=mesh['cuts'=8,'mode'=4] {'cuts','mode'}, use_global_device_ids=true, to_apply=%region_13.14 | all-reduce | flops 8 | bytes 64 | tf_op jit(solution)/shard_map/psum | solution.py:106
  252.9 15.4 %select_reduce_fusion = f32[8,4096]{1,0:T(8,128)S(1)} fusion(s32[8,4096]{1,0:T(8,128)S(1)} %get-tuple-element.23, f32[128,128,1]{1,0,2:T(8,128)S(1)} %bitcast.154, s32[8,4096]{1,0:T(8,128)S(1)} %get-tuple-element.22), kind=kOutput, calls=%fused_computation | convolution fusion | flops 6459195392 | bytes 458752 | tf_op jit(solution)/shard_map/csr,rw->csw/dot_general | solution.py:97
  268.4 0.7 multiply_divide_fusion
  269.9 123.0 %all-reduce.4.cloned.1.call-done = f32[8,4096]{1,0:T(8,128)} async-done(((f32[8,4096]{1,0:T(8,128)}), f32[8,4096]{1,0:T(8,128)}) %all-reduce.4.cloned.1.call-update) | async-done | bytes 131088 | tf_op jit(solution)/shard_map/psum | solution.py:107
  392.8 1.1 reduce_sum.55
  394.4 1.6 copy.70
  (58 shorter events, 11.4 us)
Async XLA Ops:
  7.2 111.4 %all-reduce.6.cloned.1.call-start = ((), (), s32[]{:S(2)}) async-start(), calls=%async_computation.5 | async-start | bytes 1048576 | tf_op jit(solution)/shard_map/psum | solution.py:9
  41.5 81.6 %all-to-all-start = ((bf16[8,2,4,32,2,128]{5,4,3,2,1,0:T(2,128)(2,1)}), bf16[8,2,4,32,2,128]{5,4,3,2,1,0:T(2,128)(2,1)S(1)}, u32[]{:S(2)}, u32[]{:S(2)}) async-start(bf16[8,2,4,32,2,128]{5,4,3,2,1,0:T(2,128)(2,1)} %param.4), calls=%async_computation | async-start | bytes 2097152 | tf_op jit(solution)/shard_map/all_to_all | solution.py:42
  45.8 165.8 %reduce-scatter.2.cloned.1.call-start = ((), (), s32[]{:S(2)}) async-start(), calls=%async_computation.3 | async-start | bytes 589824 | tf_op jit(solution)/shard_map/reduce_scatter | solution.py:71
  118.6 4.4 %copy-start.3 = (bf16[1,2,128,128]{3,2,0,1:T(8,128)(2,1)S(1)}, bf16[1,2,128,128]{3,2,0,1:T(8,128)(2,1)}, u32[]{:S(2)}) copy-start(bf16[1,2,128,128]{3,2,0,1:T(8,128)(2,1)} %get-tuple-element.18) | copy-start | bytes 196612
  118.6 4.4 %copy-start.2 = (bf16[1,2,128,128]{3,2,0,1:T(8,128)(2,1)S(1)}, bf16[1,2,128,128]{3,2,0,1:T(8,128)(2,1)}, u32[]{:S(2)}) copy-start(bf16[1,2,128,128]{3,2,0,1:T(8,128)(2,1)} %get-tuple-element.19) | copy-start | bytes 196612
  148.9 63.7 %copy-start.1 = (s32[8,4096]{1,0:T(8,128)S(1)}, s32[8,4096]{1,0:T(8,128)}, u32[]{:S(2)}) copy-start(s32[8,4096]{1,0:T(8,128)} %param.7) | copy-start | bytes 393220
  149.8 243.0 %all-reduce.4.cloned.1.call-start = ((), (), s32[]{:S(2)}) async-start(), calls=%async_computation.4 | async-start | bytes 262144 | tf_op jit(solution)/shard_map/psum | solution.py:107
  252.9 16.2 %copy-start = (bf16[4,32,2,128]{3,1,2,0:T(8,128)(2,1)S(1)}, bf16[4,32,2,128]{3,1,2,0:T(8,128)(2,1)}, u32[]{:S(2)}) copy-start(bf16[4,32,2,128]{3,1,2,0:T(8,128)(2,1)} %reduce-scatter.2.cloned.1.call-done) | copy-start | bytes 196612
Sparse Core Ops, SparseCore 0:
  41.6 76.9 all-reduce.5
  149.9 61.5 reduce-scatter.1
  269.3 123.5 all-reduce.3
where the time goes:
time: 403 us; the launch traced here: 402 us
  waiting for transfers between devices  257 us (64%)
  blocking collectives  51.4 us (13%)
  between operations  37.4 us (9%)
  local copies, waits for them, and re-layouts  22.5 us (6%)
  matrix products  19.5 us (5%)
  other arithmetic  9.91 us (2%)
  starting transfers between devices  4.36 us (1%)
    psum x1, waiting for transfers between devices, on_device(): lax.psum(sample_mass * dimension_scale / norm_total[:, None], ('cuts', 'm...  123 us
    psum x1, waiting for transfers between devices, from_root(): return lax.psum(jnp.where(mine, array, jnp.zeros_like(array)), axis)  72.8 us
    reduce_scatter x1, waiting for transfers between devices, on_device(): lax.psum_scatter(summed.astype(jnp.bfloat16), 'cuts', scatter_dimension=0...  61.7 us
    psum x1, blocking collectives, on_device(): norm_total = lax.psum(norm_part, ('cuts', 'mode'))  40.1 us
    dot_general x1, matrix products, on_device(): jnp.einsum('csr,rw->csw', cell_onehot, magnitude.reshape(cell_count, widt...  15.4 us
    all_to_all x1, blocking collectives, on_device(): lax.all_to_all(summed.astype(jnp.bfloat16), 'mode', split_axis=2, concat_...  11.4 us
  transfers between devices with their start and end apart: 4, of which 3 were waited for; matrix products, arithmetic and copies ran while one was open for 1% of the time, Pallas kernels for 0%

commit v1 on v0

--- a/solution.py
+++ b/solution.py
@@ -6,7 +6,7 @@
 
 def from_root(array, axis, root):
     mine = lax.axis_index(axis) == root
-    return lax.psum(jnp.where(mine, array, jnp.zeros_like(array)), axis)
+    return jnp.sum(lax.all_gather(jnp.where(mine, array, jnp.zeros_like(array)), axis), axis=0)
 
 
 def apply_gates(tensor, blocks):

time: 403 us -> 575 us (1.43)
  blocking collectives: 51.4 us -> 304 us
  waiting for transfers between devices: 257 us -> 187 us
  local copies, waits for them, and re-layouts: 22.5 us -> 14.9 us
    all_gather x0 -> x8, blocking collectives: none -> 252 us  [from_root(): lax.all_gather(jnp.where(mine, array, jnp.zeros_like(array)), axis)]
    psum x1 -> x0, waiting for transfers between devices: 72.8 us -> none  [from_root(): return lax.psum(jnp.where(mine, array, jnp.zeros_like(array)), axis)]
  transfers between devices with their start and end apart: 4 -> 3, of which waited for: 3 -> 2; matrix products, arithmetic and copies ran while one was open for 1% -> 1% of each run, Pallas kernels for 0% -> 0%
where the time goes in v1:
time: 575 us; the launch traced here: 574 us
  blocking collectives  304 us (53%)
  waiting for transfers between devices  187 us (33%)
  between operations  37.8 us (7%)
  matrix products  19.5 us (3%)
  local copies, waits for them, and re-layouts  14.9 us (3%)
  other arithmetic  6.86 us (1%)
    all_gather x8, blocking collectives, from_root(): lax.all_gather(jnp.where(mine, array, jnp.zeros_like(array)), axis)  252 us
    psum x1, waiting for transfers between devices, on_device(): lax.psum(sample_mass * dimension_scale / norm_total[:, None], ('cuts', 'm...  123 us
    reduce_scatter x1, waiting for transfers between devices, on_device(): lax.psum_scatter(summed.astype(jnp.bfloat16), 'cuts', scatter_dimension=0...  63.6 us
    psum x1, blocking collectives, on_device(): norm_total = lax.psum(norm_part, ('cuts', 'mode'))  40.1 us
    dot_general x1, matrix products, on_device(): jnp.einsum('csr,rw->csw', cell_onehot, magnitude.reshape(cell_count, widt...  15.4 us
    all_to_all x1, blocking collectives, on_device(): lax.all_to_all(summed.astype(jnp.bfloat16), 'mode', split_axis=2, concat_...  11.8 us
  transfers between devices with their start and end apart: 3, of which 2 were waited for; matrix products, arithmetic and copies ran while one was open for 1% of the time, Pallas kernels for 0%

profile of v1, /device:TPU:0, one launch (start us, length us, event | category | flops | bytes accessed | tf_op | source)
XLA Modules:
  0.0 574.0 jit_solution(6343461777723463144)
XLA Ops:
  7.2 4.4 all-to-all-start
  14.8 0.7 fusion.89
  36.4 32.6 %all_gather.32 = bf16[8,2,128,128]{3,2,1,0:T(8,128)(2,1)S(1)} all-gather(bf16[1,2,128,128]{3,2,1,0:T(8,128)(2,1)S(1)} %bitcast.149), channel_id=1, replica_groups=mesh['cuts'=8,'mode'=4] {'cuts'}, dimensions={0}, use_global_device_ids=true | all-gather | bytes 589824 | tf_op jit(solution)/shard_map/all_gather | solution.py:9
  69.6 31.5 %all_gather.33 = bf16[8,2,128,128]{3,2,1,0:T(8,128)(2,1)S(1)} all-gather(bf16[1,2,128,128]{3,2,1,0:T(8,128)(2,1)S(1)} %bitcast.150), channel_id=1, replica_groups=mesh['cuts'=8,'mode'=4] {'cuts'}, dimensions={0}, use_global_device_ids=true | all-gather | bytes 589824 | tf_op jit(solution)/shard_map/all_gather | solution.py:9
  101.6 31.4 %all_gather.34 = bf16[8,2,128,128]{3,2,1,0:T(8,128)(2,1)S(1)} all-gather(bf16[1,2,128,128]{3,2,1,0:T(8,128)(2,1)S(1)} %bitcast.151), channel_id=1, replica_groups=mesh['cuts'=8,'mode'=4] {'cuts'}, dimensions={0}, use_global_device_ids=true | all-gather | bytes 589824 | tf_op jit(solution)/shard_map/all_gather | solution.py:9
  133.4 31.2 %all_gather.35 = bf16[8,2,128,128]{3,2,1,0:T(8,128)(2,1)S(1)} all-gather(bf16[1,2,128,128]{3,2,1,0:T(8,128)(2,1)S(1)} %bitcast.152), channel_id=1, replica_groups=mesh['cuts'=8,'mode'=4] {'cuts'}, dimensions={0}, use_global_device_ids=true | all-gather | bytes 589824 | tf_op jit(solution)/shard_map/all_gather | solution.py:9
  165.0 31.5 %all_gather.36 = bf16[8,2,128,128]{3,2,1,0:T(8,128)(2,1)S(1)} all-gather(bf16[1,2,128,128]{3,2,1,0:T(8,128)(2,1)S(1)} %bitcast.153), channel_id=1, replica_groups=mesh['cuts'=8,'mode'=4] {'cuts'}, dimensions={0}, use_global_device_ids=true | all-gather | bytes 589824 | tf_op jit(solution)/shard_map/all_gather | solution.py:9
  196.9 31.3 %all_gather.37 = bf16[8,2,128,128]{3,2,1,0:T(8,128)(2,1)S(1)} all-gather(bf16[1,2,128,128]{3,2,1,0:T(8,128)(2,1)S(1)} %bitcast.154), channel_id=1, replica_groups=mesh['cuts'=8,'mode'=4] {'cuts'}, dimensions={0}, use_global_device_ids=true | all-gather | bytes 589824 | tf_op jit(solution)/shard_map/all_gather | solution.py:9
  228.6 31.4 %all_gather.38 = bf16[8,2,128,128]{3,2,1,0:T(8,128)(2,1)S(1)} all-gather(bf16[1,2,128,128]{3,2,1,0:T(8,128)(2,1)S(1)} %bitcast.155), channel_id=1, replica_groups=mesh['cuts'=8,'mode'=4] {'cuts'}, dimensions={0}, use_global_device_ids=true | all-gather | bytes 589824 | tf_op jit(solution)/shard_map/all_gather | solution.py:9
  260.4 31.4 %all_gather.39 = bf16[8,2,128,128]{3,2,1,0:T(8,128)(2,1)S(1)} all-gather(bf16[1,2,128,128]{3,2,1,0:T(8,128)(2,1)S(1)} %bitcast.156), channel_id=1, replica_groups=mesh['cuts'=8,'mode'=4] {'cuts'}, dimensions={0}, use_global_device_ids=true | all-gather | bytes 589824 | tf_op jit(solution)/shard_map/all_gather | solution.py:9
  292.0 1.2 copy.60
  293.2 0.7 reshape.385
  294.4 0.8 reshape.386
  295.2 1.1 copy.47
  296.3 0.7 reshape.387
  297.7 1.2 copy.48
  298.9 0.7 reshape.389
  300.4 1.2 copy.49
  301.6 0.7 reshape.391
  303.1 2.4 reduce_sum.154
  305.5 0.7 copy.50
  306.3 11.8 %all_to_all.33 = bf16[2,4,128,2,128]{4,3,1,0,2:T(2,128)(2,1)S(1)} all-to-all(bf16[2,4,128,2,128]{4,3,1,0,2:T(2,128)(2,1)S(1)} %copy.50), channel_id=1, replica_groups=mesh['cuts'=8,'mode'=4] {'mode'}, dimensions={2} | all-to-all | bytes 1048576 | tf_op jit(solution)/shard_map/all_to_all | solution.py:66
  318.2 0.9 copy.52
  319.2 63.6 %reduce-scatter.2.cloned.1.call-done = bf16[4,32,2,128]{3,1,2,0:T(8,128)(2,1)} async-done(((bf16[32,32,2,128]{3,1,2,0:T(8,128)(2,1)}), bf16[4,32,2,128]{3,1,2,0:T(8,128)(2,1)}) %reduce-scatter.2.cloned.1.call-update) | async-done | bytes 65552 | tf_op jit(solution)/shard_map/reduce_scatter | solution.py:71
  382.8 0.8 convert_element_type.93
  384.1 40.1 %psum.14 = f32[8]{0:T(128)S(1)} all-reduce(f32[8]{0:T(128)S(1)} %select_reduce_fusion.1), channel_id=1, replica_groups=mesh['cuts'=8,'mode'=4] {'cuts','mode'}, use_global_device_ids=true, to_apply=%region_13.14 | all-reduce | flops 8 | bytes 64 | tf_op jit(solution)/shard_map/psum | solution.py:106
  424.2 15.4 %select_reduce_fusion = f32[8,4096]{1,0:T(8,128)S(1)} fusion(s32[8,4096]{1,0:T(8,128)S(1)} %get-tuple-element.26, f32[128,128,1]{1,0,2:T(8,128)S(1)} %bitcast.174, s32[8,4096]{1,0:T(8,128)S(1)} %get-tuple-element.25), kind=kOutput, calls=%fused_computation | convolution fusion | flops 6459195392 | bytes 458752 | tf_op jit(solution)/shard_map/csr,rw->csw/dot_general | solution.py:97
  439.6 0.7 multiply_divide_fusion
  440.4 0.7 copy.54
  441.1 122.9 %all-reduce.2.cloned.1.call-done = f32[8,4096]{1,0:T(8,128)} async-done(((f32[8,4096]{1,0:T(8,128)}), f32[8,4096]{1,0:T(8,128)}) %all-reduce.2.cloned.1.call-update) | async-done | bytes 131088 | tf_op jit(solution)/shard_map/psum | solution.py:107
  564.0 1.1 reduce_sum.159
  565.6 1.6 copy.63
  (64 shorter events, 8.0 us)
Async XLA Ops:
  7.2 7.7 %copy-start.3 = (s32[32]{0:T(128)S(1)}, s32[32]{0:T(128)}, u32[]{:S(2)}) copy-start(s32[32]{0:T(128)} %param.6) | copy-start | bytes 388
  7.2 28.7 %copy-start.1 = (bf16[4,2,128,128]{3,2,1,0:T(8,128)(2,1)S(1)}, bf16[4,2,128,128]{3,2,1,0:T(8,128)(2,1)}, u32[]{:S(2)}) copy-start(bf16[4,2,128,128]{3,2,1,0:T(8,128)(2,1)} %param.5) | copy-start | bytes 786436
  7.2 284.8 %all-to-all-start = ((bf16[8,2,4,32,2,128]{5,4,3,2,1,0:T(2,128)(2,1)}), bf16[8,2,4,32,2,128]{5,4,3,2,1,0:T(2,128)(2,1)S(1)}, u32[]{:S(2)}, u32[]{:S(2)}) async-start(bf16[8,2,4,32,2,128]{5,4,3,2,1,0:T(2,128)(2,1)} %param.4), calls=%async_computation | async-start | bytes 2097152 | tf_op jit(solution)/shard_map/all_to_all | solution.py:42
  11.6 371.2 %reduce-scatter.2.cloned.1.call-start = ((), (), s32[]{:S(2)}) async-start(), calls=%async_computation.3 | async-start | bytes 589824 | tf_op jit(solution)/shard_map/reduce_scatter | solution.py:71
  318.2 65.6 %copy-start.2 = (s32[8,4096]{1,0:T(8,128)S(1)}, s32[8,4096]{1,0:T(8,128)}, u32[]{:S(2)}) copy-start(s32[8,4096]{1,0:T(8,128)} %param.7) | copy-start | bytes 393220
  319.1 244.9 %all-reduce.2.cloned.1.call-start = ((), (), s32[]{:S(2)}) async-start(), calls=%async_computation.4 | async-start | bytes 262144 | tf_op jit(solution)/shard_map/psum | solution.py:107
  424.2 16.2 %copy-start = (bf16[4,32,2,128]{3,1,2,0:T(8,128)(2,1)S(1)}, bf16[4,32,2,128]{3,1,2,0:T(8,128)(2,1)}, u32[]{:S(2)}) copy-start(bf16[4,32,2,128]{3,1,2,0:T(8,128)(2,1)} %reduce-scatter.2.cloned.1.call-done) | copy-start | bytes 196612
Sparse Core Ops, SparseCore 0:
  319.2 63.5 reduce-scatter.1
  440.5 123.4 all-reduce.1
